TPU v7x, 256 devices: a whole 4x4x8 slice. The times are simulated.
256 devices in a mesh: seq: 64 (over x, z, core), head: 4 (over y).
Axes of the slice: x: 4, y: 4, z: 8, core: 2. Of those that a mesh axis runs over, the one named last changes fastest.
Arguments:
- queries: bfloat16 [16384, 64, 128], P('seq', 'head'), may hold values from -360 to 360
- head_weights: bfloat16 [16384, 64], P('seq', 'head'), may hold values from -0.75 to 0.75
- keys: bfloat16 [16384, 128], P('seq'), may hold values from -6 to 6
- targets: bfloat16 [16384, 2048], P('seq'), may hold values from 0.0099487305 to 10
- chosen: int32 [128, 16], P('seq'), may hold values from -1 to 127, as said below
- tile_block: int32 [128], replicated, may hold values from 0 to 127, as said below
Outputs:
- query_grads: bfloat16 [16384, 64, 128], P('seq', 'head')
- weight_grads: float32 [16384, 64], P('seq', 'head')
- key_grads: float32 [16384, 128], P('seq')
- loss: float32 [], replicated
Inputs may be any that keep to these rules, and one draw needn't show every extreme that they name: `tile_block`: a permutation of 0 to 127; each aligned group of 4 stored positions holds the global blocks of that same group. `chosen`: slot 0 of stored tile p is tile_block[p]; live entries of a row are distinct, none exceeds tile_block[p], and they precede the -1 entries; over all tiles of one device of seq, at most 1 distinct live block is stored on any one other device.
All inputs are finite; a program needn't handle non-finite values.
Results may differ from a plain program's by a relative error of at most 0.0095.
Values may be sent and summed in bfloat16 or wider, within the bound.
A program may use at most 128 MiB of HBM per device.

v0:
```python
import jax
import jax.numpy as jnp
from jax import lax
from jax.sharding import Mesh
from jax.sharding import PartitionSpec as P

BLOCK = 128
SLOTS = 16
CAP = 1
KEYS = 2048
SEQ = ("seq_0", "seq_1", "seq_2")
SEQ_HEAD = ("seq_0", "seq_1", "seq_2", "head")
loss_scale = 4194304.0


def over_axes(value, axes):
    for axis in axes:
        value = lax.psum(value, axis)
    return value


def copy_for_each(value, axis):
    copies = jnp.broadcast_to(value, (lax.axis_size(axis), *value.shape))
    return lax.all_to_all(copies, axis, split_axis=0, concat_axis=0, tiled=True)


def over_copies(value, axis):
    return copy_for_each(value, axis).astype(jnp.float32).sum(axis=0)


def row_statistics(score_part, mask_part, target_part):
    row_max = jnp.max(jnp.where(mask_part, score_part, -1e30), axis=1)
    exp_terms = jnp.where(
        mask_part, jnp.exp(jnp.where(mask_part, score_part - row_max[:, None], 0.0)), 0.0
    )
    return (row_max, jnp.sum(exp_terms, axis=1), jnp.sum(target_part, axis=1))


def local(queries, head_weights, keys, targets, chosen, tile_block):
    row_count, heads_here, key_width = queries.shape
    tiles_here = row_count // BLOCK
    block_count = tile_block.shape[0]
    owner_count = block_count // tiles_here
    score_scale = key_width ** (-0.5)
    seq_index = lax.axis_index(SEQ)
    head_index = lax.axis_index("head")
    is_first = (head_index == 0).astype(jnp.float32)
    positions = jnp.arange(block_count, dtype=jnp.int32)
    home_of = jnp.sum(
        jnp.where(tile_block[None, :] == positions[:, None], positions[None, :], 0), axis=1
    )
    live_slot = chosen >= 0
    position = home_of[jnp.maximum(chosen, 0)]
    owner_index = position // tiles_here
    local_slot = position % tiles_here
    own_block = lax.dynamic_slice_in_dim(tile_block, seq_index * tiles_here, tiles_here)
    offsets = jnp.arange(BLOCK, dtype=jnp.int32)
    causal = offsets[None, :] <= offsets[:, None]
    own_slot = chosen == own_block[:, None]
    live_mask = live_slot[:, None, :, None] & (
        (~own_slot)[:, None, :, None] | causal[None, :, None, :]
    )
    live_mask = live_mask.reshape(row_count, KEYS)
    key_blocks = keys.reshape(tiles_here, BLOCK, key_width)
    remote = live_slot & (owner_index != seq_index)
    remote_pos = jnp.where(remote, position, -1).reshape(-1)
    wanted = jnp.any(remote_pos[:, None] == positions[None, :], axis=0).reshape(
        owner_count, tiles_here
    )
    slot_rank = jnp.cumsum(wanted.astype(jnp.int32), axis=1) - 1
    local_iota = jnp.arange(tiles_here, dtype=jnp.int32)
    request = jnp.stack(
        [jnp.sum(jnp.where(wanted & (slot_rank == 0), local_iota[None, :], 0), axis=1)], axis=1
    )
    asked_slots = lax.all_to_all(request, SEQ, split_axis=0, concat_axis=0, tiled=True)
    reply_blocks = key_blocks[asked_slots]
    arrived = lax.all_to_all(reply_blocks, SEQ, split_axis=0, concat_axis=0, tiled=True)
    key_table = jnp.concatenate(
        [key_blocks, arrived.reshape(owner_count * CAP, BLOCK, key_width)], axis=0
    )
    table_index = jnp.where(
        owner_index == seq_index,
        local_slot,
        tiles_here + owner_index * CAP + slot_rank[owner_index, local_slot],
    )
    table_index = jnp.where(live_slot, table_index, 0)
    fetched = key_table[table_index]
    query_tiles = queries.reshape(tiles_here, BLOCK, heads_here, key_width)
    weight_tiles = head_weights.astype(jnp.float32).reshape(tiles_here, BLOCK, heads_here)

    def dot_values(query_tile, key_tile):
        return jnp.einsum(
            "qhd,kd->qhk",
            query_tile,
            key_tile.reshape(-1, key_width),
            preferred_element_type=jnp.float32,
        )

    def forward(operands):
        query_tile, weight_tile, key_tile = operands
        values = dot_values(query_tile, key_tile)
        return score_scale * jnp.sum(jnp.maximum(values, 0.0) * weight_tile[:, :, None], axis=1)

    partial_value = lax.map(forward, (query_tiles, weight_tiles, fetched)).reshape(row_count, KEYS)
    target_vals = jnp.where(live_mask, targets.astype(jnp.float32), 0.0)
    pair_local = jnp.sum(live_mask.astype(jnp.float32))
    score_part = lax.psum(partial_value, "head")
    row_max, row_norm, row_target = row_statistics(score_part, live_mask, target_vals)
    target_prob = jnp.where(live_mask, target_vals / row_target[:, None], 0.0)
    kl_cols = jnp.sum(
        jnp.where(
            live_mask,
            target_prob * (jnp.log(jnp.where(live_mask, target_prob, 1.0)) - score_part),
            0.0,
        )
    )
    lse_sum = jnp.sum(row_max + jnp.log(row_norm))
    loss_part = is_first * (kl_cols + lse_sum)
    loss_total, pair_count = (
        over_axes(loss_part, SEQ_HEAD),
        over_axes(is_first * pair_local, SEQ_HEAD),
    )
    softmax_vals = (
        jnp.where(live_mask, jnp.exp(jnp.where(live_mask, score_part - row_max[:, None], 0.0)), 0.0)
        / row_norm[:, None]
    )
    grad_part = loss_scale * KEYS * (softmax_vals - target_prob) / pair_count
    grad_tiles = grad_part.reshape(tiles_here, BLOCK, KEYS)

    def backward(operands):
        query_tile, weight_tile, key_tile, grad_tile = operands
        key_rows = key_tile.reshape(-1, key_width)
        values = dot_values(query_tile, key_tile)
        weight_grad = score_scale * jnp.sum(
            jnp.maximum(values, 0.0) * grad_tile[:, None, :], axis=2
        )
        dot_grads = (
            score_scale
            * weight_tile[:, :, None]
            * grad_tile[:, None, :]
            * (values > 0).astype(jnp.float32)
        ).astype(jnp.bfloat16)
        query_grad = jnp.einsum(
            "qhk,kd->qhd", dot_grads, key_rows, preferred_element_type=jnp.float32
        ).astype(jnp.bfloat16)
        key_grad = jnp.einsum(
            "qhk,qhd->kd", dot_grads, query_tile, preferred_element_type=jnp.float32
        )
        return (query_grad, weight_grad, key_grad.reshape(SLOTS, BLOCK, key_width))

    query_grads, weight_grads, key_parts = lax.map(
        backward, (query_tiles, weight_tiles, fetched, grad_tiles)
    )
    slot_grads = key_parts.reshape(tiles_here * SLOTS, BLOCK, key_width)
    spread = jax.ops.segment_sum(
        slot_grads, table_index.reshape(-1), num_segments=tiles_here + owner_count * CAP
    )
    returned = lax.all_to_all(
        spread[tiles_here:].reshape(owner_count, CAP, BLOCK, key_width).astype(jnp.bfloat16),
        SEQ,
        split_axis=0,
        concat_axis=0,
        tiled=True,
    ).astype(jnp.float32)
    owned_grad = spread[:tiles_here] + jax.ops.segment_sum(
        returned.reshape(owner_count * CAP, BLOCK, key_width),
        asked_slots.reshape(-1),
        num_segments=tiles_here,
    )
    key_grads = over_copies(owned_grad.astype(jnp.bfloat16), "head").astype(jnp.float32)
    return (
        query_grads.reshape(row_count, heads_here, key_width),
        weight_grads.reshape(row_count, heads_here),
        key_grads.reshape(row_count, key_width),
        KEYS * loss_total / pair_count,
    )


def solution(mesh):
    torus = Mesh(
        mesh.devices.reshape(4, 8, 2, mesh.shape["head"]), ("seq_0", "seq_1", "seq_2", "head")
    )
    in_specs = (P(SEQ, "head", None), P(SEQ, "head"), P(SEQ, None), P(SEQ, None), P(SEQ, None), P())
    out_specs = (P(SEQ, "head", None), P(SEQ, "head"), P(SEQ, None), P())
    return jax.shard_map(local, mesh=torus, in_specs=in_specs, out_specs=out_specs, check_vma=False)
```

profile of v0, /device:TPU:1, one launch (start us, length us, event | category | flops | bytes accessed | tf_op | source)
XLA Modules:
  0.0 379.5 jit_solution(12548023386545640363)
XLA Ops:
  7.2 0.8 select_reduce_fusion.2
  8.0 0.7 broadcast_maximum_fusion
  8.8 0.7 gather_fusion
  9.5 0.7 and_select_fusion.3
  10.3 0.1 fusion.41
  10.4 0.2 reshape.231
  10.6 0.2 reduce_window_sum.11
  10.7 0.1 broadcast_add_fusion
  10.9 0.1 copy.39
  11.0 22.1 %all_to_all.27 = s32[64,1,1]{2,1,0:T(1,128)S(1)} all-to-all(s32[64,1,1]{2,1,0:T(1,128)S(1)} %copy.39), channel_id=1, replica_groups=mesh['seq_0'=4,'seq_1'=8,'seq_2'=2,'head'=4] {'seq_0','seq_1','seq_2'}, dimensions={0} | all-to-all | bytes 512 | tf_op jit(solution)/shard_map/all_to_all | solution.py:75
  33.1 2.7 fusion.46
  35.8 2.2 gather_fusion.1
  37.9 5.7 %all-to-all-start.1 = ((bf16[64,1,128,128]{3,2,1,0:T(8,128)(2,1)}), bf16[64,1,128,128]{3,2,1,0:T(8,128)(2,1)}, u32[]{:S(2)}, u32[]{:S(2)}) async-start(bf16[64,1,128,128]{3,2,1,0:T(8,128)(2,1)} %bitcast.22), calls=%async_computation.1 | async-start | bytes 4194304 | tf_op jit(solution)/shard_map/all_to_all | solution.py:77
  43.9 0.7 gather_fusion.2
  44.8 0.3 copy.42
  45.1 49.8 %all-to-all-done.1 = bf16[64,1,128,128]{3,2,1,0:T(8,128)(2,1)} async-done(((bf16[64,1,128,128]{3,2,1,0:T(8,128)(2,1)}), bf16[64,1,128,128]{3,2,1,0:T(8,128)(2,1)}, u32[]{:S(2)}, u32[]{:S(2)}) %all-to-all-start.1) | async-done | bytes 2097184 | tf_op jit(solution)/shard_map/all_to_all | solution.py:77
  94.9 3.1 pad_maximum_fusion
  98.0 2.4 gather_fusion.3
  100.4 8.3 %while.24 = (s32[]{:T(128)}, f32[2,128,2048]{2,1,0:T(8,128)}, bf16[2,128,16,128]{3,1,2,0:T(8,128)(2,1)S(1)}, bf16[2,16,128,128]{3,2,1,0:T(8,128)(2,1)S(1)}, f32[2,128,16]{1,2,0:T(8,128)S(1)}, /*index=5*/s32[]{:T(128)}) while((s32[]{:T(128)}, f32[2,128,2048]{2,1,0:T(8,128)}, bf16[2,128,16,128]{3,1,2,0:T(8,128)(2,1)S(1)}, ...), condition=%wide.region_6.7_spmd, body=%wide.region_4.6_spmd.sunk | while | flops 1086324736 | bytes 22044820 | solution.py:104
  100.5 2.6 multiply_reduce_fusion.4
  103.1 0.1 bitcast_dynamic-update-slice_fusion.2
  103.3 1.3 copy-done.8
  104.6 2.6 multiply_reduce_fusion.4
  107.3 0.1 bitcast_dynamic-update-slice_fusion.2
  107.4 1.3 copy-done.8
  108.8 0.6 copy-done.14
  109.5 1.3 convert_reduce_fusion
  111.5 1.2 or_and_fusion
  112.7 56.5 %all-reduce.6.cloned.1.call-done = f32[256,2048]{1,0:T(8,128)} async-done(((f32[256,2048]{1,0:T(8,128)}), f32[256,2048]{1,0:T(8,128)}) %all-reduce.6.cloned.1.call-update) | async-done | bytes 2097168 | tf_op jit(solution)/shard_map/psum | solution.py:107
  169.2 2.9 select_reduce_fusion.1
  172.1 3.6 select_reduce_fusion
  175.7 0.7 add_reduce_fusion
  177.8 0.6 reshape.279
  178.4 8.9 %all-reduce.2 = (f32[]{:T(128)}, f32[]{:T(128)}) all-reduce(f32[]{:T(128)S(6)} %mul.113, f32[]{:T(128)S(6)} %mul.115), channel_id=1, replica_groups=mesh['seq_0'=4,'seq_1'=8,'seq_2'=2,'head'=4] {'seq_0'}, use_global_device_ids=true, to_apply=%region_12.13 | all-reduce | flops 2 | bytes 16 | tf_op jit(solution)/shard_map/psum | solution.py:18
  187.3 14.4 %all-reduce = (f32[]{:T(128)}, f32[]{:T(128)}) all-reduce(f32[]{:T(128)} %get-tuple-element.167, f32[]{:T(128)} %get-tuple-element.168), channel_id=1, replica_groups=mesh['seq_0'=4,'seq_1'=8,'seq_2'=2,'head'=4] {'seq_1'}, use_global_device_ids=true, to_apply=%region_13.14 | all-reduce | flops 2 | bytes 16 | tf_op jit(solution)/shard_map/psum | solution.py:18
  201.7 9.4 %all-reduce.3 = (f32[]{:T(128)}, f32[]{:T(128)}) all-reduce(f32[]{:T(128)} %get-tuple-element.163, f32[]{:T(128)} %get-tuple-element.164), channel_id=1, replica_groups=mesh['seq_0'=4,'seq_1'=8,'seq_2'=2,'head'=4] {'seq_2'}, use_global_device_ids=true, to_apply=%region_14.15 | all-reduce | flops 2 | bytes 16 | tf_op jit(solution)/shard_map/psum | solution.py:18
  211.1 7.4 %all-reduce.1 = (f32[]{:T(128)}, f32[]{:T(128)}) all-reduce(f32[]{:T(128)} %get-tuple-element.169, f32[]{:T(128)} %get-tuple-element.170), channel_id=1, replica_groups=mesh['seq_0'=4,'seq_1'=8,'seq_2'=2,'head'=4] {'head'}, use_global_device_ids=true, to_apply=%region_15.16 | all-reduce | flops 2 | bytes 16 | tf_op jit(solution)/shard_map/psum | solution.py:18
  218.4 4.8 %multiply_divide_fusion = f32[256,2048]{1,0:T(8,128)} fusion(f32[256,2048]{1,0:T(8,128)S(1)} %copy-done.1, bf16[256,2048]{1,0:T(8,128)(2,1)} %param.13, f32[]{:T(128)} %get-tuple-element.165, f32[256]{0:T(256)S(1)} %get-tuple-element.134, f32[256]{0:T(256)S(1)} %get-tuple-element.132, f32[256]{0:T(256)S(1)} %get-tuple-element.133, ...), kind=kLoop, calls=%fused_computation.54 | loop fusion | flops 5767168 | bytes 5770244 | tf_op jit(solution)/shard_map/div | solution.py:127
  223.2 54.7 %while.25 = (s32[]{:T(128)}, bf16[2,128,16,128]{3,2,1,0:T(8,128)(2,1)}, f32[2,128,16]{1,0,2:T(2,128)S(1)}, f32[2,16,128,128]{3,2,1,0:T(8,128)}, bf16[2,128,16,12...) while((s32[]{:T(128)}, ...), condition=%wide.region_18.19_spmd, body=%wide.region_16.18_spmd.sunk | while | flops 3313502208 | bytes 53560508 | solution.py:151
  223.3 1.6 dynamic-slice_bitcast_fusion.6
  224.9 7.1 %fusion.74 = (u16[128,2048]{1,0:T(8,128)(2,1)S(1)}, f32[128,16,2048]{2,0,1:T(8,128)}) fusion(bf16[2048,128,1]{1,0,2:T(8,128)(2,1)S(1)} %bitcast.149, bf16[2,128,16,128]{3,1,2,0:T(8,128)(2,1)S(1)} %copy-done.4, s32[]{:T(128)S(6)} %copy.100), kind=kOutput, calls=%fused_computation.21.clone.1 | convolution fusion | flops 1094451200 | bytes 18350084 | tf_op jit(solution)/shard_map/while/body/eval_jaxpr/qhd,kd->qhk/dot_general | solution.py:92
  232.0 3.4 fusion.75
  235.4 7.5 %multiply_reduce_fusion.5 = f32[128,16]{0,1:T(8,128)S(1)} fusion(f32[128,16,2048]{2,0,1:T(8,128)} %get-tuple-element.272, f32[128,2048]{1,0:T(8,128)S(1)} %get-tuple-element.269), kind=kLoop, calls=%fused_computation.19.clone.1 | loop fusion | flops 12580864 | bytes 17833984 | tf_op jit(solution)/shard_map/while/body/eval_jaxpr/reduce_sum | solution.py:134
  243.0 2.2 copy_dynamic-update-slice_fusion.2
  245.1 5.4 %fusion.76 = f32[2,16,128,128]{3,2,1,0:T(8,128)} fusion(f32[2,16,128,128]{3,2,1,0:T(8,128)} %get-tuple-element.306, s32[]{:T(128)S(6)} %copy.100, bf16[2,128,16,128]{3,1,2,0:T(8,128)(2,1)} %get-tuple-element.317, f32[2048,128]{0,1:T(8,128)S(1)} %get-tuple-element.273, f32[16,128]{1,0:T(8,128)S(1)} %get-tuple-element.274, u16[128,2048]{1,0:T(8,128)(2,1)} %copy-done.2), kind=kOutput, calls=%fused_computation.28.clone.1 | convolution fusion | flops 1103101952 | bytes 3154944 | tf_op jit(solution)/shard_map/while/body/eval_jaxpr/qhk,qhd->kd/dot_general | solution.py:146
  250.6 1.6 dynamic-slice_bitcast_fusion.6
  252.2 7.1 %fusion.74 = (u16[128,2048]{1,0:T(8,128)(2,1)S(1)}, f32[128,16,2048]{2,0,1:T(8,128)}) fusion(bf16[2048,128,1]{1,0,2:T(8,128)(2,1)S(1)} %bitcast.149, bf16[2,128,16,128]{3,1,2,0:T(8,128)(2,1)S(1)} %copy-done.4, s32[]{:T(128)S(6)} %copy.100), kind=kOutput, calls=%fused_computation.21.clone.1 | convolution fusion | flops 1094451200 | bytes 18350084 | tf_op jit(solution)/shard_map/while/body/eval_jaxpr/qhd,kd->qhk/dot_general | solution.py:92
  259.4 3.4 fusion.75
  262.8 7.5 %multiply_reduce_fusion.5 = f32[128,16]{0,1:T(8,128)S(1)} fusion(f32[128,16,2048]{2,0,1:T(8,128)} %get-tuple-element.272, f32[128,2048]{1,0:T(8,128)S(1)} %get-tuple-element.269), kind=kLoop, calls=%fused_computation.19.clone.1 | loop fusion | flops 12580864 | bytes 17833984 | tf_op jit(solution)/shard_map/while/body/eval_jaxpr/reduce_sum | solution.py:134
  270.3 2.2 copy_dynamic-update-slice_fusion.2
  272.5 5.4 %fusion.76 = f32[2,16,128,128]{3,2,1,0:T(8,128)} fusion(f32[2,16,128,128]{3,2,1,0:T(8,128)} %get-tuple-element.306, s32[]{:T(128)S(6)} %copy.100, bf16[2,128,16,128]{3,1,2,0:T(8,128)(2,1)} %get-tuple-element.317, f32[2048,128]{0,1:T(8,128)S(1)} %get-tuple-element.273, f32[16,128]{1,0:T(8,128)S(1)} %get-tuple-element.274, u16[128,2048]{1,0:T(8,128)(2,1)} %copy-done.2), kind=kOutput, calls=%fused_computation.28.clone.1 | convolution fusion | flops 1103101952 | bytes 3154944 | tf_op jit(solution)/shard_map/while/body/eval_jaxpr/qhk,qhd->kd/dot_general | solution.py:146
  277.9 2.5 broadcast_in_dim.112
  280.5 6.9 %scatter_fusion = f32[66,128,128]{2,1,0:T(8,128)} fusion(f32[66,128,128]{2,1,0:T(8,128)} %broadcast_in_dim.112, s32[32]{0:T(128)S(1)} %copy-done.13, f32[32,128,128]{2,1,0:T(8,128)S(1)} %bitcast.157), kind=kCustom, calls=%fused_computation.4 | custom fusion | flops 524288 | bytes 6291584 | tf_op jit(solution)/shard_map/scatter-add | solution.py:155
  287.4 3.9 %fusion.37 = bf16[64,1,128,128]{3,2,1,0:T(8,128)(2,1)} fusion(f32[66,128,128]{2,1,0:T(8,128)} %scatter_fusion), kind=kLoop, calls=%fused_computation.50 | loop fusion | bytes 4194304 | tf_op jit(solution)/shard_map/convert_element_type | solution.py:159
  291.3 6.9 %all-to-all-start.2 = ((bf16[64,1,128,128]{3,2,1,0:T(8,128)(2,1)}), bf16[64,1,128,128]{3,2,1,0:T(8,128)(2,1)S(1)}, u32[]{:S(2)}, u32[]{:S(2)}) async-start(bf16[64,1,128,128]{3,2,1,0:T(8,128)(2,1)} %fusion.37), calls=%async_computation.2 | async-start | bytes 4194304 | tf_op jit(solution)/shard_map/all_to_all | solution.py:158
  298.2 0.9 slice.17
  299.2 50.3 %all-to-all-done.2 = bf16[64,1,128,128]{3,2,1,0:T(8,128)(2,1)S(1)} async-done(((bf16[64,1,128,128]{3,2,1,0:T(8,128)(2,1)}), bf16[64,1,128,128]{3,2,1,0:T(8,128)(2,1)S(1)}, u32[]{:S(2)}, u32[]{:S(2)}) %all-to-all-start.2) | async-done | bytes 2097184 | tf_op jit(solution)/shard_map/all_to_all | solution.py:158
  349.4 2.5 bitcast_convert_fusion
  351.9 8.8 %scatter_fusion.1 = f32[2,128,128]{2,1,0:T(8,128)S(1)} fusion(f32[2,128,128]{2,1,0:T(8,128)S(1)} %slice.17, s32[64]{0:T(128)S(1)} %copy-done.12, f32[64,128,128]{2,1,0:T(8,128)} %bitcast_convert_fusion), kind=kCustom, calls=%fused_computation.5 | custom fusion | flops 1048576 | bytes 12583168 | tf_op jit(solution)/shard_map/scatter-add | solution.py:165
  360.7 0.7 broadcast_in_dim.113
  361.4 3.4 all-to-all-start.3
  366.2 0.6 copy.80
  366.8 4.1 %all-to-all-done.3 = bf16[4,2,128,128]{3,2,1,0:T(8,128)(2,1)S(1)} async-done(((bf16[4,2,128,128]{3,2,1,0:T(8,128)(2,1)}), bf16[4,2,128,128]{3,2,1,0:T(8,128)(2,1)S(1)}, u32[]{:S(2)}, u32[]{:S(2)}) %all-to-all-start.3) | async-done | bytes 262176 | tf_op jit(solution)/shard_map/all_to_all | solution.py:24
  370.9 0.7 convert_reduce_fusion.1
  (71 shorter events, 1.2 us)
Async XLA Ops:
  7.2 28.6 %copy-start = (bf16[256,128]{1,0:T(8,128)(2,1)S(1)}, bf16[256,128]{1,0:T(8,128)(2,1)}, u32[]{:S(2)}) copy-start(bf16[256,128]{1,0:T(8,128)(2,1)} %param.12) | copy-start | bytes 196612
  37.9 6.9 %copy-start.9 = (bf16[256,16,128]{2,1,0:T(8,128)(2,1)S(1)}, bf16[256,16,128]{2,1,0:T(8,128)(2,1)}, u32[]{:S(2)}) copy-start(bf16[256,16,128]{2,1,0:T(8,128)(2,1)} %param.10) | copy-start | bytes 3145732
  37.9 57.0 %all-to-all-start.1 = ((bf16[64,1,128,128]{3,2,1,0:T(8,128)(2,1)}), bf16[64,1,128,128]{3,2,1,0:T(8,128)(2,1)}, u32[]{:S(2)}, u32[]{:S(2)}) async-start(bf16[64,1,128,128]{3,2,1,0:T(8,128)(2,1)} %bitcast.22), calls=%async_computation.1 | async-start | bytes 4194304 | tf_op jit(solution)/shard_map/all_to_all | solution.py:77
  43.7 1.4 copy-start.11
  43.7 125.5 %all-reduce.6.cloned.1.call-start = ((), (), s32[]{:S(2)}) async-start(), calls=%async_computation.4 | async-start | bytes 4194304 | tf_op jit(solution)/shard_map/psum | solution.py:107
  100.5 2.7 copy-start.7
  103.3 1.3 copy-start.8
  104.6 2.7 copy-start.7
  107.4 1.3 copy-start.8
  108.7 3.9 %copy-start.3 = (bf16[2,128,16,128]{3,1,2,0:T(8,128)(2,1)}, bf16[2,128,16,128]{3,1,2,0:T(8,128)(2,1)S(1)}, u32[]{:S(2)}) copy-start(bf16[2,128,16,128]{3,1,2,0:T(8,128)(2,1)S(1)} %get-tuple-element.326) | copy-start | bytes 3145732
  108.7 0.7 copy-start.14
  108.7 0.7 copy-start.10
  169.2 2.9 copy-start.1
  169.2 2.9 copy-start.5
  223.2 1.6 copy-start.4
  232.0 3.4 copy-start.2
  250.6 1.6 copy-start.4
  259.4 3.4 copy-start.2
  277.9 2.5 copy-start.6
  277.9 2.5 copy-start.13
  291.3 58.1 %all-to-all-start.2 = ((bf16[64,1,128,128]{3,2,1,0:T(8,128)(2,1)}), bf16[64,1,128,128]{3,2,1,0:T(8,128)(2,1)S(1)}, u32[]{:S(2)}, u32[]{:S(2)}) async-start(bf16[64,1,128,128]{3,2,1,0:T(8,128)(2,1)} %fusion.37), calls=%async_computation.2 | async-start | bytes 4194304 | tf_op jit(solution)/shard_map/all_to_all | solution.py:158
  299.1 52.7 %copy-start.12 = (s32[64]{0:T(128)S(1)}, s32[64]{0:T(128)}, u32[]{:S(2)}) copy-start(s32[64]{0:T(128)} %get-tuple-element.135) | copy-start | bytes 772
  361.4 9.4 %all-to-all-start.3 = ((bf16[4,2,128,128]{3,2,1,0:T(8,128)(2,1)}), bf16[4,2,128,128]{3,2,1,0:T(8,128)(2,1)S(1)}, u32[]{:S(2)}, u32[]{:S(2)}) async-start(bf16[4,2,128,128]{3,2,1,0:T(8,128)(2,1)} %broadcast_in_dim.113), calls=%async_computation.3 | async-start | bytes 524288 | tf_op jit(solution)/shard_map/all_to_all | solution.py:24
Sparse Core Ops, SparseCore 0:
  108.9 60.2 all-reduce.5
where the time goes:
time: 381 us; the launch traced here: 380 us
  waiting for transfers between devices  161 us (42%)
  blocking collectives  62.1 us (16%)
  other arithmetic  57.1 us (15%)
  matrix products  37.2 us (10%)
  local copies, waits for them, and re-layouts  27.4 us (7%)
  between operations  18.7 us (5%)
  starting transfers between devices  16.1 us (4%)
    psum x1, waiting for transfers between devices, local(): score_part = lax.psum(partial_value, 'head')  56.5 us
    all_to_all x1, waiting for transfers between devices, local(): lax.all_to_all(spread[tiles_here:].reshape(owner_count, CAP, BLOCK, key_w...  50.3 us
    all_to_all x1, waiting for transfers between devices, local(): lax.all_to_all(reply_blocks, SEQ, split_axis=0, concat_axis=0, tiled=True)  49.8 us
    psum x4, blocking collectives, over_axes(): value = lax.psum(value, axis)  40 us
    all_to_all x1, blocking collectives, local(): lax.all_to_all(request, SEQ, split_axis=0, concat_axis=0, tiled=True)  22.1 us
    dot_general x4, matrix products, dot_values(): jnp.einsum('qhd,kd->qhk', query_tile, key_tile.reshape(-1, key_width), pr...  19.5 us
    reduce_sum x2, other arithmetic, backward(): jnp.sum(jnp.maximum(values, 0.0) * grad_tile[:, None, :], axis=2)  14.9 us
    dot_general x2, matrix products, backward(): jnp.einsum('qhk,qhd->kd', dot_grads, query_tile, preferred_element_type=j...  10.9 us
  transfers between devices with their start and end apart: 4, of which 4 were waited for; matrix products, arithmetic and copies ran while one was open for 1% of the time, Pallas kernels for 0%

commit v1 on v0

--- a/solution.py
+++ b/solution.py
@@ -15,7 +15,8 @@
 
 def over_axes(value, axes):
     for axis in axes:
-        value = lax.psum(value, axis)
+        pieces = lax.all_gather(value, axis, axis=0, tiled=False)
+        value = pieces.sum(axis=0)
     return value
 
 

time: 381 us -> 394 us (1.034)
  local copies, waits for them, and re-layouts: 27.4 us -> 39.6 us
  other arithmetic: 57.1 us -> 61.9 us
    psum x4 -> x0, blocking collectives: 40 us -> none  [over_axes(): value = lax.psum(value, axis)]
    unnamed x0 -> x4, blocking collectives: none -> 37.8 us
    unnamed x23 -> x53, local copies, waits for them, and re-layouts: 1.24 us -> 13.4 us
    reduce_sum x0 -> x8, other arithmetic: none -> 4.85 us  [over_axes(): value = pieces.sum(axis=0)]
  transfers between devices with their start and end apart: 4 -> 4, of which waited for: 4 -> 4; matrix products, arithmetic and copies ran while one was open for 1% -> 2% of each run, Pallas kernels for 0% -> 0%
where the time goes in v1:
time: 394 us; the launch traced here: 392 us
  waiting for transfers between devices  159 us (40%)
  other arithmetic  61.9 us (16%)
  blocking collectives  59.9 us (15%)
  local copies, waits for them, and re-layouts  39.6 us (10%)
  matrix products  37.2 us (9%)
  between operations  18.8 us (5%)
  starting transfers between devices  16.1 us (4%)
    psum x1, waiting for transfers between devices, local(): score_part = lax.psum(partial_value, 'head')  55.2 us
    all_to_all x1, waiting for transfers between devices, local(): lax.all_to_all(spread[tiles_here:].reshape(owner_count, CAP, BLOCK, key_w...  50.3 us
    all_to_all x1, waiting for transfers between devices, local(): lax.all_to_all(reply_blocks, SEQ, split_axis=0, concat_axis=0, tiled=True)  49.8 us
    unnamed x4, blocking collectives  37.8 us
    all_to_all x1, blocking collectives, local(): lax.all_to_all(request, SEQ, split_axis=0, concat_axis=0, tiled=True)  22.1 us
    dot_general x4, matrix products, dot_values(): jnp.einsum('qhd,kd->qhk', query_tile, key_tile.reshape(-1, key_width), pr...  19.5 us
    reduce_sum x2, other arithmetic, backward(): jnp.sum(jnp.maximum(values, 0.0) * grad_tile[:, None, :], axis=2)  14.9 us
    unnamed x53, local copies, waits for them, and re-layouts  13.4 us
  transfers between devices with their start and end apart: 4, of which 4 were waited for; matrix products, arithmetic and copies ran while one was open for 2% of the time, Pallas kernels for 0%

profile of v1, /device:TPU:1, one launch (start us, length us, event | category | flops | bytes accessed | tf_op | source)
XLA Modules:
  0.0 392.4 jit_solution(16988501009234976717)
XLA Ops:
  7.2 0.8 select_reduce_fusion.2
  8.0 0.7 broadcast_maximum_fusion
  8.8 0.7 gather_fusion
  9.5 0.7 and_select_fusion.3
  11.0 22.1 %all_to_all.27 = s32[64,1,1]{2,1,0:T(1,128)S(1)} all-to-all(s32[64,1,1]{2,1,0:T(1,128)S(1)} %copy.39), channel_id=1, replica_groups=mesh['seq_0'=4,'seq_1'=8,'seq_2'=2,'head'=4] {'seq_0','seq_1','seq_2'}, dimensions={0} | all-to-all | bytes 512 | tf_op jit(solution)/shard_map/all_to_all | solution.py:76
  33.1 2.7 fusion.46
  35.8 2.2 gather_fusion.1
  38.0 5.7 %all-to-all-start.1 = ((bf16[64,1,128,128]{3,2,1,0:T(8,128)(2,1)}), bf16[64,1,128,128]{3,2,1,0:T(8,128)(2,1)}, u32[]{:S(2)}, u32[]{:S(2)}) async-start(bf16[64,1,128,128]{3,2,1,0:T(8,128)(2,1)} %bitcast.22), calls=%async_computation.1 | async-start | bytes 4194304 | tf_op jit(solution)/shard_map/all_to_all | solution.py:78
  43.9 0.7 gather_fusion.2
  45.1 49.8 %all-to-all-done.1 = bf16[64,1,128,128]{3,2,1,0:T(8,128)(2,1)} async-done(((bf16[64,1,128,128]{3,2,1,0:T(8,128)(2,1)}), bf16[64,1,128,128]{3,2,1,0:T(8,128)(2,1)}, u32[]{:S(2)}, u32[]{:S(2)}) %all-to-all-start.1) | async-done | bytes 2097184 | tf_op jit(solution)/shard_map/all_to_all | solution.py:78
  94.9 3.1 pad_maximum_fusion
  98.0 2.4 gather_fusion.3
  100.4 8.3 %while.24 = (s32[]{:T(128)}, f32[2,128,2048]{2,1,0:T(8,128)}, bf16[2,128,16,128]{3,1,2,0:T(8,128)(2,1)S(1)}, bf16[2,16,128,128]{3,2,1,0:T(8,128)(2,1)S(1)}, f32[2,128,16]{1,2,0:T(8,128)S(1)}, /*index=5*/s32[]{:T(128)}) while((s32[]{:T(128)}, f32[2,128,2048]{2,1,0:T(8,128)}, bf16[2,128,16,128]{3,1,2,0:T(8,128)(2,1)S(1)}, ...), condition=%wide.region_6.7_spmd, body=%wide.region_4.6_spmd.sunk | while | flops 1086324736 | bytes 22044820 | solution.py:105
  100.5 2.6 multiply_reduce_fusion.4
  103.3 1.3 copy-done.8
  104.6 2.6 multiply_reduce_fusion.4
  107.4 1.3 copy-done.8
  110.2 1.3 convert_reduce_fusion
  112.1 0.7 dynamic-update-slice
  112.8 1.2 or_and_fusion
  114.0 55.2 %all-reduce.14.cloned.1.call-done = f32[256,2048]{1,0:T(8,128)} async-done(((f32[256,2048]{1,0:T(8,128)}), f32[256,2048]{1,0:T(8,128)}) %all-reduce.14.cloned.1.call-update) | async-done | bytes 2097168 | tf_op jit(solution)/shard_map/psum | solution.py:108
  169.2 2.9 select_reduce_fusion.1
  172.1 3.6 select_reduce_fusion
  175.8 0.7 add_reduce_fusion
  177.8 0.7 dynamic-update-slice.4
  178.6 0.6 dynamic-slice.1
  179.2 8.4 %all-reduce.10 = (f32[4]{0:T(128)S(1)}, f32[4]{0:T(128)S(1)}) all-reduce(f32[4]{0:T(128)S(1)} %dynamic-update-slice, f32[4]{0:T(128)S(1)} %dynamic-update-slice.4), channel_id=1, replica_groups=mesh['seq_0'=4,'seq_1'=8,'seq_2'=2,'head'=4] {'seq_0'}, use_global_device_ids=true, to_apply=%add | all-reduce | flops 8 | bytes 64
  188.8 1.3 dynamic-update-slice.5
  190.1 1.4 dynamic-update-slice.1
  191.5 0.6 dynamic-slice.2
  192.1 13.7 %all-reduce.8 = (f32[8]{0:T(128)S(1)}, f32[8]{0:T(128)S(1)}) all-reduce(f32[8]{0:T(128)S(1)} %dynamic-update-slice.1, f32[8]{0:T(128)S(1)} %dynamic-update-slice.5), channel_id=1, replica_groups=mesh['seq_0'=4,'seq_1'=8,'seq_2'=2,'head'=4] {'seq_1'}, use_global_device_ids=true, to_apply=%add.1 | all-reduce | flops 16 | bytes 128
  207.0 1.3 dynamic-update-slice.6
  208.3 1.5 dynamic-update-slice.2
  210.5 8.7 %all-reduce.11 = (f32[2]{0:T(128)S(1)}, f32[2]{0:T(128)S(1)}) all-reduce(f32[2]{0:T(128)S(1)} %dynamic-update-slice.2, f32[2]{0:T(128)S(1)} %dynamic-update-slice.6), channel_id=1, replica_groups=mesh['seq_0'=4,'seq_1'=8,'seq_2'=2,'head'=4] {'seq_2'}, use_global_device_ids=true, to_apply=%add.2 | all-reduce | flops 4 | bytes 32
  220.4 1.3 dynamic-update-slice.7
  221.7 1.4 dynamic-update-slice.3
  223.7 7.0 %all-reduce.9 = (f32[4]{0:T(128)S(1)}, f32[4]{0:T(128)}) all-reduce(f32[4]{0:T(128)S(1)} %dynamic-update-slice.3, f32[4]{0:T(128)S(1)} %dynamic-update-slice.7), channel_id=1, replica_groups=mesh['seq_0'=4,'seq_1'=8,'seq_2'=2,'head'=4] {'head'}, use_global_device_ids=true, to_apply=%add.3 | all-reduce | flops 8 | bytes 64
  230.7 0.6 reduce_sum.170
  231.3 4.8 %multiply_divide_fusion = f32[256,2048]{1,0:T(8,128)} fusion(f32[256,2048]{1,0:T(8,128)S(1)} %copy-done.1, bf16[256,2048]{1,0:T(8,128)(2,1)} %param.13, f32[]{:T(128)} %reduce_sum.170, f32[256]{0:T(256)S(1)} %get-tuple-element.134, f32[256]{0:T(256)S(1)} %get-tuple-element.132, f32[256]{0:T(256)S(1)} %get-tuple-element.133, pred[32,8,16,128]{3,2,1,0:T(8,128)(4,1)} %bitcast.167), kind=kLoop, calls=%fused_computation.54 | loop fusion | flops 5767168 | bytes 5770244 | tf_op jit(solution)/shard_map/div | solution.py:128
  236.1 54.8 %while.25 = (s32[]{:T(128)}, bf16[2,128,16,128]{3,2,1,0:T(8,128)(2,1)}, f32[2,128,16]{1,0,2:T(2,128)S(1)}, f32[2,16,128,128]{3,2,1,0:T(8,128)}, bf16[2,128,16,12...) while((s32[]{:T(128)}, ...), condition=%wide.region_18.19_spmd, body=%wide.region_16.18_spmd.sunk | while | flops 3313502208 | bytes 53560508 | solution.py:152
  236.1 1.6 dynamic-slice_bitcast_fusion.6
  237.8 7.1 %fusion.74 = (u16[128,2048]{1,0:T(8,128)(2,1)S(1)}, f32[128,16,2048]{2,0,1:T(8,128)}) fusion(bf16[2048,128,1]{1,0,2:T(8,128)(2,1)S(1)} %bitcast.161, bf16[2,128,16,128]{3,1,2,0:T(8,128)(2,1)S(1)} %copy-done.4, s32[]{:T(128)S(6)} %copy.116), kind=kOutput, calls=%fused_computation.21.clone.1 | convolution fusion | flops 1094451200 | bytes 18350084 | tf_op jit(solution)/shard_map/while/body/eval_jaxpr/qhd,kd->qhk/dot_general | solution.py:93
  244.9 3.4 fusion.75
  248.3 7.5 %multiply_reduce_fusion.5 = f32[128,16]{0,1:T(8,128)S(1)} fusion(f32[128,16,2048]{2,0,1:T(8,128)} %get-tuple-element.272, f32[128,2048]{1,0:T(8,128)S(1)} %get-tuple-element.269), kind=kLoop, calls=%fused_computation.19.clone.1 | loop fusion | flops 12580864 | bytes 17833984 | tf_op jit(solution)/shard_map/while/body/eval_jaxpr/reduce_sum | solution.py:135
  255.8 2.2 copy_dynamic-update-slice_fusion.2
  258.0 5.4 %fusion.76 = f32[2,16,128,128]{3,2,1,0:T(8,128)} fusion(f32[2,16,128,128]{3,2,1,0:T(8,128)} %get-tuple-element.306, s32[]{:T(128)S(6)} %copy.116, bf16[2,128,16,128]{3,1,2,0:T(8,128)(2,1)} %get-tuple-element.317, f32[2048,128]{0,1:T(8,128)S(1)} %get-tuple-element.273, f32[16,128]{1,0:T(8,128)S(1)} %get-tuple-element.274, u16[128,2048]{1,0:T(8,128)(2,1)} %copy-done.2), kind=kOutput, calls=%fused_computation.28.clone.1 | convolution fusion | flops 1103101952 | bytes 3154944 | tf_op jit(solution)/shard_map/while/body/eval_jaxpr/qhk,qhd->kd/dot_general | solution.py:147
  263.5 1.6 dynamic-slice_bitcast_fusion.6
  265.1 7.1 %fusion.74 = (u16[128,2048]{1,0:T(8,128)(2,1)S(1)}, f32[128,16,2048]{2,0,1:T(8,128)}) fusion(bf16[2048,128,1]{1,0,2:T(8,128)(2,1)S(1)} %bitcast.161, bf16[2,128,16,128]{3,1,2,0:T(8,128)(2,1)S(1)} %copy-done.4, s32[]{:T(128)S(6)} %copy.116), kind=kOutput, calls=%fused_computation.21.clone.1 | convolution fusion | flops 1094451200 | bytes 18350084 | tf_op jit(solution)/shard_map/while/body/eval_jaxpr/qhd,kd->qhk/dot_general | solution.py:93
  272.2 3.4 fusion.75
  275.6 7.5 %multiply_reduce_fusion.5 = f32[128,16]{0,1:T(8,128)S(1)} fusion(f32[128,16,2048]{2,0,1:T(8,128)} %get-tuple-element.272, f32[128,2048]{1,0:T(8,128)S(1)} %get-tuple-element.269), kind=kLoop, calls=%fused_computation.19.clone.1 | loop fusion | flops 12580864 | bytes 17833984 | tf_op jit(solution)/shard_map/while/body/eval_jaxpr/reduce_sum | solution.py:135
  283.2 2.2 copy_dynamic-update-slice_fusion.2
  285.4 5.5 %fusion.76 = f32[2,16,128,128]{3,2,1,0:T(8,128)} fusion(f32[2,16,128,128]{3,2,1,0:T(8,128)} %get-tuple-element.306, s32[]{:T(128)S(6)} %copy.116, bf16[2,128,16,128]{3,1,2,0:T(8,128)(2,1)} %get-tuple-element.317, f32[2048,128]{0,1:T(8,128)S(1)} %get-tuple-element.273, f32[16,128]{1,0:T(8,128)S(1)} %get-tuple-element.274, u16[128,2048]{1,0:T(8,128)(2,1)} %copy-done.2), kind=kOutput, calls=%fused_computation.28.clone.1 | convolution fusion | flops 1103101952 | bytes 3154944 | tf_op jit(solution)/shard_map/while/body/eval_jaxpr/qhk,qhd->kd/dot_general | solution.py:147
  290.9 2.5 broadcast_in_dim.112
  293.4 6.9 %scatter_fusion = f32[66,128,128]{2,1,0:T(8,128)} fusion(f32[66,128,128]{2,1,0:T(8,128)} %broadcast_in_dim.112, s32[32]{0:T(128)S(1)} %copy-done.13, f32[32,128,128]{2,1,0:T(8,128)S(1)} %bitcast.169), kind=kCustom, calls=%fused_computation.4 | custom fusion | flops 524288 | bytes 6291584 | tf_op jit(solution)/shard_map/scatter-add | solution.py:156
  300.3 3.9 fusion.37
  304.2 6.9 %all-to-all-start.2 = ((bf16[64,1,128,128]{3,2,1,0:T(8,128)(2,1)}), bf16[64,1,128,128]{3,2,1,0:T(8,128)(2,1)S(1)}, u32[]{:S(2)}, u32[]{:S(2)}) async-start(bf16[64,1,128,128]{3,2,1,0:T(8,128)(2,1)} %fusion.37), calls=%async_computation.2 | async-start | bytes 4194304 | tf_op jit(solution)/shard_map/all_to_all | solution.py:159
  311.1 0.9 slice.17
  312.1 50.3 %all-to-all-done.2 = bf16[64,1,128,128]{3,2,1,0:T(8,128)(2,1)S(1)} async-done(((bf16[64,1,128,128]{3,2,1,0:T(8,128)(2,1)}), bf16[64,1,128,128]{3,2,1,0:T(8,128)(2,1)S(1)}, u32[]{:S(2)}, u32[]{:S(2)}) %all-to-all-start.2) | async-done | bytes 2097184 | tf_op jit(solution)/shard_map/all_to_all | solution.py:159
  362.3 2.5 bitcast_convert_fusion
  364.8 8.8 %scatter_fusion.1 = f32[2,128,128]{2,1,0:T(8,128)S(1)} fusion(f32[2,128,128]{2,1,0:T(8,128)S(1)} %slice.17, s32[64]{0:T(128)S(1)} %copy-done.12, f32[64,128,128]{2,1,0:T(8,128)} %bitcast_convert_fusion), kind=kCustom, calls=%fused_computation.5 | custom fusion | flops 1048576 | bytes 12583168 | tf_op jit(solution)/shard_map/scatter-add | solution.py:166
  373.6 0.7 broadcast_in_dim.113
  374.3 3.4 all-to-all-start.3
  380.3 3.5 all-to-all-done.3
  383.8 0.7 convert_reduce_fusion.1
  (109 shorter events, 9.6 us)
Async XLA Ops:
  7.2 28.6 %copy-start = (bf16[256,128]{1,0:T(8,128)(2,1)S(1)}, bf16[256,128]{1,0:T(8,128)(2,1)}, u32[]{:S(2)}) copy-start(bf16[256,128]{1,0:T(8,128)(2,1)} %param.12) | copy-start | bytes 196612
  37.9 6.9 %copy-start.9 = (bf16[256,16,128]{2,1,0:T(8,128)(2,1)S(1)}, bf16[256,16,128]{2,1,0:T(8,128)(2,1)}, u32[]{:S(2)}) copy-start(bf16[256,16,128]{2,1,0:T(8,128)(2,1)} %param.10) | copy-start | bytes 3145732
  38.0 57.0 %all-to-all-start.1 = ((bf16[64,1,128,128]{3,2,1,0:T(8,128)(2,1)}), bf16[64,1,128,128]{3,2,1,0:T(8,128)(2,1)}, u32[]{:S(2)}, u32[]{:S(2)}) async-start(bf16[64,1,128,128]{3,2,1,0:T(8,128)(2,1)} %bitcast.22), calls=%async_computation.1 | async-start | bytes 4194304 | tf_op jit(solution)/shard_map/all_to_all | solution.py:78
  43.7 1.4 copy-start.11
  43.7 125.5 %all-reduce.14.cloned.1.call-start = ((), (), s32[]{:S(2)}) async-start(), calls=%async_computation.4 | async-start | bytes 4194304 | tf_op jit(solution)/shard_map/psum | solution.py:108
  100.5 2.7 copy-start.7
  103.3 1.3 copy-start.8
  104.6 2.7 copy-start.7
  107.4 1.3 copy-start.8
  108.7 5.3 %copy-start.3 = (bf16[2,128,16,128]{3,1,2,0:T(8,128)(2,1)}, bf16[2,128,16,128]{3,1,2,0:T(8,128)(2,1)S(1)}, u32[]{:S(2)}) copy-start(bf16[2,128,16,128]{3,1,2,0:T(8,128)(2,1)S(1)} %get-tuple-element.326) | copy-start | bytes 3145732
  108.7 0.7 copy-start.14
  108.7 0.7 copy-start.18
  108.7 1.3 copy-start.10
  169.2 2.9 copy-start.1
  169.2 2.9 copy-start.5
  172.1 6.5 %copy-start.17 = (u32[256]{0:T(256)S(1)}, u32[256]{0:T(256)}, u32[]{:S(2)}) copy-start(u32[256]{0:T(256)} %constant.152) | copy-start | bytes 3076
  172.1 19.4 %copy-start.16 = (u32[256]{0:T(256)S(1)}, u32[256]{0:T(256)}, u32[]{:S(2)}) copy-start(u32[256]{0:T(256)} %constant.157) | copy-start | bytes 3076
  172.1 37.7 %copy-start.15 = (u32[256]{0:T(256)S(1)}, u32[256]{0:T(256)}, u32[]{:S(2)}) copy-start(u32[256]{0:T(256)} %constant.162) | copy-start | bytes 3076
  236.1 1.6 copy-start.4
  244.9 3.4 copy-start.2
  263.5 1.6 copy-start.4
  272.2 3.4 copy-start.2
  290.9 2.5 copy-start.6
  290.9 2.5 copy-start.13
  304.2 58.1 %all-to-all-start.2 = ((bf16[64,1,128,128]{3,2,1,0:T(8,128)(2,1)}), bf16[64,1,128,128]{3,2,1,0:T(8,128)(2,1)S(1)}, u32[]{:S(2)}, u32[]{:S(2)}) async-start(bf16[64,1,128,128]{3,2,1,0:T(8,128)(2,1)} %fusion.37), calls=%async_computation.2 | async-start | bytes 4194304 | tf_op jit(solution)/shard_map/all_to_all | solution.py:159
  312.0 52.7 %copy-start.12 = (s32[64]{0:T(128)S(1)}, s32[64]{0:T(128)}, u32[]{:S(2)}) copy-start(s32[64]{0:T(128)} %get-tuple-element.135) | copy-start | bytes 772
  364.8 12.9 %copy-start.19 = (f32[4]{0:T(128)S(1)}, f32[4]{0:T(128)}, u32[]{:S(2)}) copy-start(f32[4]{0:T(128)} %get-tuple-element.166) | copy-start | bytes 52
  374.3 9.4 %all-to-all-start.3 = ((bf16[4,2,128,128]{3,2,1,0:T(8,128)(2,1)}), bf16[4,2,128,128]{3,2,1,0:T(8,128)(2,1)S(1)}, u32[]{:S(2)}, u32[]{:S(2)}) async-start(bf16[4,2,128,128]{3,2,1,0:T(8,128)(2,1)} %broadcast_in_dim.113), calls=%async_computation.3 | async-start | bytes 524288 | tf_op jit(solution)/shard_map/all_to_all | solution.py:25
Sparse Core Ops, SparseCore 0:
  108.9 60.2 all-reduce.13
